TPU v7x, 32 devices: a whole 2x2x4 slice. The times are simulated.
32 devices in a mesh: dp: 16 (over z, y, x), shard: 2 (over core).
Axes of the slice: x: 2, y: 2, z: 4, core: 2. Of those that a mesh axis runs over, the one named last changes fastest.
Arguments:
- features: bfloat16 [65536, 1024], P('dp'), may hold values from -150 to 150
- shared_weight: bfloat16 [1024, 2048], P(None, 'shard'), may hold values from -0.1875 to 0.1875
- task_heads: bfloat16 [6, 2048], P(None, 'shard'), may hold values from -0.4 to 0.4
- labels: int32 [65536, 6], P('dp'), may hold values from 0 to 1
- task_masks: int32 [65536, 6], P('dp'), may hold values from 0 to 1
- task_weights: float32 [6], replicated, may hold values from 0.5 to 2
- initial_losses: float32 [6], replicated, may hold values from 0.2 to 1
Outputs:
- update: float32 [1024, 2048], P('dp', 'shard')
- new_weights: float32 [6], replicated
All inputs are finite; a program needn't handle non-finite values.
Results may differ from a plain program's by a relative error of at most 0.00089.
Values sent between devices are 32-bit elements; how exact they have to be, the bound alone decides.
No kernel may reach another device: no remote copies, remote signals or barrier semaphores. Data moves between devices by JAX's collectives and lax.ppermute only.
A program may use at most 256 MiB of HBM per device.

v0:
```python
import jax
import jax.numpy as jnp
from jax import lax
from jax.sharding import PartitionSpec as P

epsilon = 1e-06
learn_rate = 0.5
asymmetry = 1.5


def silu_parts(preact):
    sigmoid_pre = jax.nn.sigmoid(preact)
    return (preact * sigmoid_pre, sigmoid_pre * (1.0 + preact * (1.0 - sigmoid_pre)))


def renew_weights(losses, squares, task_weights, initial_losses, entries):
    root_mean = jnp.sqrt(squares / entries + epsilon)
    scaled = task_weights * root_mean
    average = jnp.mean(scaled)
    loss_ratio = losses / initial_losses
    relative = loss_ratio / jnp.mean(loss_ratio)
    target = average * relative**asymmetry
    distance = (scaled - target) / average
    raised = task_weights * jnp.exp(-learn_rate * distance)
    return raised.shape[0] * raised / jnp.sum(raised)


def task_term(inputs, terms):
    return lax.dot_general(
        inputs, terms, (((0,), (0,)), ((), ())), preferred_element_type=jnp.float32
    )


def local_gram(gradients):
    return jnp.einsum("rtc,rsc->ts", gradients, gradients, precision=lax.Precision.HIGHEST)


def weighted_sum(new_weights, gradients):
    return jnp.einsum("t,rtc->rc", new_weights, gradients, precision=lax.Precision.HIGHEST)


def quadratic(gram_total, new_weights):
    inner = jnp.dot(gram_total, new_weights, precision=lax.Precision.HIGHEST)
    return jnp.dot(new_weights, inner, precision=lax.Precision.HIGHEST)


def on_device(
    features, shared_weight, task_heads, labels, task_masks, task_weights, initial_losses
):
    shard_count = lax.axis_size("shard")
    replica_count = lax.axis_size("dp")
    sample_count = features.shape[0]
    width_in = features.shape[1]
    local_hidden = shared_weight.shape[1]
    task_count = task_heads.shape[0]
    entries = width_in * local_hidden * shard_count
    total_samples = sample_count * replica_count
    own_rows = width_in // replica_count
    preact = jnp.dot(features, shared_weight, preferred_element_type=jnp.float32)
    activated, silu_slope = silu_parts(preact)
    hidden = activated.astype(jnp.bfloat16)
    partial_logits = lax.dot_general(
        hidden, task_heads, (((1,), (1,)), ((), ())), preferred_element_type=jnp.float32
    )
    logits = lax.psum(partial_logits, "shard")
    targets = labels.astype(jnp.float32)
    mask_float = task_masks.astype(jnp.float32)
    loss_part = (
        jnp.sum(mask_float * (jax.nn.softplus(logits) - targets * logits), axis=0) / total_samples
    )
    errors = mask_float * (jax.nn.sigmoid(logits) - targets)
    back_terms = (
        errors[:, :, None] * silu_slope[:, None, :] * task_heads.astype(jnp.float32)[None]
    ).astype(jnp.bfloat16)
    losses = lax.psum(loss_part, "dp")
    flat_terms = back_terms.reshape(sample_count, task_count * local_hidden)
    gradients = lax.psum_scatter(
        task_term(features, flat_terms), "dp", scatter_dimension=0, tiled=True
    )
    gradients = gradients.reshape(own_rows, task_count, local_hidden)
    gram_total = lax.psum(local_gram(gradients), ("dp", "shard"))
    new_weights = renew_weights(
        losses, jnp.diagonal(gram_total), task_weights, initial_losses, entries
    )
    combined = weighted_sum(new_weights, gradients)
    mean_square = quadratic(gram_total, new_weights) / entries
    update = combined * lax.rsqrt(mean_square + epsilon)
    return (update, new_weights)


def solution(mesh):
    return jax.shard_map(
        on_device,
        mesh=mesh,
        in_specs=(
            P("dp", None),
            P(None, "shard"),
            P(None, "shard"),
            P("dp", None),
            P("dp", None),
            P(),
            P(),
        ),
        out_specs=(P("dp", "shard"), P()),
        check_vma=False,
    )
```

profile of v0, /device:TPU:0, one launch (start us, length us, event | category | flops | bytes accessed | tf_op | source)
XLA Modules:
  0.0 675.0 jit_solution(6087586694705920439)
XLA Ops:
  7.2 0.0 copy-start
  7.2 0.0 copy-start.4
  7.2 0.0 all-reduce.2.cloned.1.call-start
  7.2 1.5 copy-done
  8.8 21.6 %add_multiply_fusion = (f32[4096,1024]{1,0:T(8,128)}, f32[4096,1024]{1,0:T(8,128)}) fusion(bf16[4096,1024]{1,0:T(8,128)(2,1)} %param.7, bf16[1024,1024]{1,0:T(8,128)(2,1)S(1)} %copy-done), kind=kOutput, calls=%fused_computation.4 | convolution fusion | flops 8619294720 | bytes 44040192 | tf_op jit(solution)/shard_map/dot_general | solution.py:59
  30.4 0.0 copy-done.4
  30.4 8.7 %fusion.1 = f32[4096,6]{0,1:T(8,128)} fusion(bf16[6,1024]{1,0:T(8,128)(2,1)S(1)} %copy-done.4, f32[4096,1024]{1,0:T(8,128)} %get-tuple-element.7), kind=kOutput, calls=%fused_computation.8 | convolution fusion | flops 71303168 | bytes 16887808 | tf_op jit(solution)/shard_map/dot_general | solution.py:62
  39.1 0.0 all-reduce.2.cloned.1.call-update
  39.1 0.2 reduce-scatter.4.cloned.1.call-start
  39.4 0.0 copy-start.2
  39.4 0.0 copy-start.3
  39.4 17.5 %copy.15 = f32[4096,1024]{0,1:T(8,128)} copy(f32[4096,1024]{1,0:T(8,128)} %get-tuple-element.6) | data formatting | bytes 33554432 | tf_op jit(solution)/shard_map/mul | solution.py:13
  57.0 3.0 all-reduce.2.cloned.1.call-done
  59.9 0.0 copy-done.2
  59.9 0.0 copy-done.3
  59.9 1.7 fusion.6
  61.6 49.7 %broadcast_multiply_fusion = f32[4096,6,1024]{0,2,1:T(8,128)} fusion(f32[4096,1024]{0,1:T(8,128)} %copy.15, f32[4096,6]{0,1:T(8,128)S(1)} %get-tuple-element.5), kind=kLoop, calls=%fused_computation.3 | loop fusion | flops 25165824 | bytes 117538816 | tf_op jit(solution)/shard_map/mul | solution.py:73
  111.3 48.2 %fusion = bf16[4096,6144]{0,1:T(8,128)(2,1)} fusion(f32[4096,6,1024]{0,2,1:T(8,128)} %broadcast_multiply_fusion, f32[6144]{0:T(1024)S(1)} %reshape.18), kind=kLoop, calls=%fused_computation.2 | loop fusion | flops 50331648 | bytes 151019520 | tf_op jit(solution)/shard_map/convert_element_type | solution.py:74
  159.5 60.6 %convolution_bitcast_fusion = f32[1024,6144]{0,1:T(8,128)} fusion(bf16[4096,6144]{0,1:T(8,128)(2,1)} %fusion, bf16[4096,1024]{1,0:T(8,128)(2,1)} %param.7), kind=kOutput, calls=%fused_computation.7 | convolution fusion | flops 51539607552 | bytes 83886080 | tf_op jit(solution)/shard_map/dot_general | solution.py:29
  220.1 24.7 %copy.21 = f32[1024,6144]{1,0:T(8,128)} copy(f32[1024,6144]{0,1:T(8,128)} %convolution_bitcast_fusion) | data formatting | bytes 50331648
  244.8 0.0 copy-start.6
  244.8 0.0 copy-start.8
  244.8 0.0 copy-start.1
  244.8 0.0 copy-start.7
  244.8 0.0 reduce-scatter.4.cloned.1.call-update
  244.8 0.6 copy-done.6
  245.4 44.1 %psum.23 = f32[6]{0:T(128)S(1)} all-reduce(f32[6]{0:T(128)S(1)} %broadcast_multiply_fusion.1), channel_id=1, replica_groups=mesh['dp'=16,'shard'=2] {'dp'}, use_global_device_ids=true, to_apply=%region_5.6 | all-reduce | flops 6 | bytes 48 | tf_op jit(solution)/shard_map/psum | solution.py:75
  289.5 0.0 copy-done.8
  289.5 0.6 divide_reduce_fusion
  290.2 314.8 %reduce-scatter.4.cloned.1.call-done = f32[64,6144]{1,0:T(8,128)} async-done(((f32[1024,6144]{1,0:T(8,128)}), f32[64,6144]{1,0:T(8,128)}) %reduce-scatter.4.cloned.1.call-update) | async-done | bytes 1572880
  605.0 3.3 copy.22
  608.3 4.0 copy.16
  612.3 7.0 %convolution_bitcast_fusion.1 = f32[6,6]{1,0:T(8,128)S(1)} fusion(f32[64,6,1024]{2,1,0:T(8,128)} %copy.16), kind=kOutput, calls=%fused_computation.9 | convolution fusion | flops 28311552 | bytes 1573008 | tf_op jit(solution)/shard_map/rtc,rsc->ts/dot_general | solution.py:35
  620.0 39.3 %psum.22 = f32[6,6]{1,0:T(8,128)S(1)} all-reduce(f32[6,6]{1,0:T(8,128)S(1)} %convolution_bitcast_fusion.1), channel_id=1, replica_groups=mesh['dp'=16,'shard'=2] {'dp','shard'}, use_global_device_ids=true, to_apply=%region_2.3 | all-reduce | flops 36 | bytes 288 | tf_op jit(solution)/shard_map/psum | solution.py:81
  659.3 0.6 gather_fusion
  660.0 0.0 copy-done.7
  660.0 0.6 fusion.11
  661.3 0.6 fusion.12
  661.9 0.6 multiply_divide_fusion
  662.5 0.0 copy-start.5
  662.6 0.7 fusion.3
  663.3 3.4 fusion.8
  667.4 0.8 bitcast_multiply_fusion.1
  668.1 0.0 copy-done.5
  668.1 0.0 copy-done.1
  (3 shorter events, 0.0 us)
Async XLA Ops:
  7.2 1.6 copy-start
  7.2 23.2 %copy-start.4 = (bf16[6,1024]{1,0:T(8,128)(2,1)S(1)}, bf16[6,1024]{1,0:T(8,128)(2,1)}, u32[]{:S(2)}) copy-start(bf16[6,1024]{1,0:T(8,128)(2,1)} %param.9) | copy-start | bytes 36868
  7.2 52.7 %all-reduce.2.cloned.1.call-start = ((), (), s32[]{:S(2)}) async-start(), calls=%async_computation.1 | async-start | bytes 262144 | tf_op jit(solution)/shard_map/psum | solution.py:65
  39.1 565.8 %reduce-scatter.4.cloned.1.call-start = ((), (), s32[]{:S(2)}) async-start(), calls=%async_computation.2 | async-start | bytes 26738688
  39.4 20.5 %copy-start.2 = (s32[4096,6]{0,1:T(8,128)S(1)}, s32[4096,6]{0,1:T(8,128)}, u32[]{:S(2)}) copy-start(s32[4096,6]{0,1:T(8,128)} %param.10) | copy-start | bytes 294916
  39.4 20.5 %copy-start.3 = (s32[4096,6]{0,1:T(8,128)S(1)}, s32[4096,6]{0,1:T(8,128)}, u32[]{:S(2)}) copy-start(s32[4096,6]{0,1:T(8,128)} %param.11) | copy-start | bytes 294916
  244.8 0.7 copy-start.6
  244.8 44.8 %copy-start.8 = (f32[6]{0:T(128)S(1)}, f32[6]{0:T(128)}, u32[]{:S(2)}) copy-start(f32[6]{0:T(128)} %param.13) | copy-start | bytes 76
  244.8 423.4 %copy-start.1 = (bf16[1024,1024]{1,0:T(8,128)(2,1)S(1)}, bf16[1024,1024]{1,0:T(8,128)(2,1)}, u32[]{:S(2)}) copy-start(bf16[1024,1024]{1,0:T(8,128)(2,1)} %param.8) | copy-start | bytes 6291460
  244.8 415.2 %copy-start.7 = (f32[6]{0:T(128)S(1)}, f32[6]{0:T(128)}, u32[]{:S(2)}) copy-start(f32[6]{0:T(128)} %param.12) | copy-start | bytes 76
  662.5 5.6 copy-start.5
Sparse Core Ops, SparseCore 0:
  39.3 20.6 all-reduce.1
  244.9 360.0 reduce-scatter.3
where the time goes:
time: 676 us; the launch traced here: 675 us
  waiting for transfers between devices  318 us (47%)
  other arithmetic  103 us (15%)
  matrix products  102 us (15%)
  blocking collectives  83.4 us (12%)
  local copies, waits for them, and re-layouts  52.4 us (8%)
  between operations  16.1 us (2%)
    unnamed x3, waiting for transfers between devices  315 us
    dot_general x1, matrix products, task_term(): lax.dot_general(inputs, terms, (((0,), (0,)), ((), ())), preferred_elemen...  60.6 us
    mul x1, other arithmetic, on_device(): errors[:, :, None] * silu_slope[:, None, :]  49.7 us
    convert_element_type x1, other arithmetic, on_device(): back_terms = (errors[:, :, None] * silu_slope[:, None, :] * task_heads.as...  48.2 us
    psum x1, blocking collectives, on_device(): losses = lax.psum(loss_part, 'dp')  44.1 us
    psum x1, blocking collectives, on_device(): gram_total = lax.psum(local_gram(gradients), ('dp', 'shard'))  39.3 us
    unnamed x20, local copies, waits for them, and re-layouts  30.2 us
    dot_general x1, matrix products, on_device(): jnp.dot(features, shared_weight, preferred_element_type=jnp.float32)  21.6 us
  transfers between devices with their start and end apart: 2, of which 2 were waited for; matrix products, arithmetic and copies ran while one was open for 3% of the time, Pallas kernels for 0%

commit v1 on v0

v1 whole, which is shorter than its diff:
```python
import functools
import jax
import jax.numpy as jnp
from jax import lax
from jax.experimental import pallas as pl
from jax.experimental.pallas import tpu as pltpu
from jax.sharding import PartitionSpec as P

epsilon = 1e-06
learn_rate = 0.5
LANES = 128
SUBLANES = 8
MIB = 1 << 20


def xor_pairs(count, bit):
    return [(place, place ^ (1 << bit)) for place in range(count)]


def split_orders(bits, tasks):
    if bits == 4:
        base = [tuple(int(letter) for letter in name) for name in SPLITS]
    else:
        base = [tuple((start + step) % bits for step in range(bits)) for start in range(bits)]
    return [base[task % len(base)] for task in range(tasks)]


SPLITS = ("1023", "0123", "2103", "1023", "0123", "2013")


def front_body(place_ref, x_ref, w_ref, heads_ref, slope_ref, logits_ref, turned_ref):
    place = place_ref[0]
    rows = turned_ref.shape[1]
    x = x_ref[...]
    block = x.shape[0]
    here = pl.ds(pl.multiple_of(pl.program_id(0) * block, block), block)
    preact = jnp.dot(x, w_ref[...], preferred_element_type=jnp.float32)
    sigmoid_pre = jax.nn.sigmoid(preact)
    slope_ref[here] = sigmoid_pre * (1.0 + preact * (1.0 - sigmoid_pre))
    hidden = (preact * sigmoid_pre).astype(jnp.bfloat16)
    partial = lax.dot_general(
        hidden, heads_ref[...], (((1,), (1,)), ((), ())), preferred_element_type=jnp.float32
    )
    logits_ref[:, here] = partial.T[:SUBLANES]
    for tile in range(x.shape[1] // LANES):
        turned = x[:, tile * LANES : (tile + 1) * LANES].T
        for part in range(LANES // rows):
            spot = jnp.bitwise_xor(place, tile * (LANES // rows) + part)
            turned_ref[spot, :, here] = turned[part * rows : (part + 1) * rows]


def front(place, features, shared_weight, heads, replicas, block=512):
    samples, width_in = features.shape
    local_hidden = shared_weight.shape[1]
    rows = width_in // replicas
    resident = pl.BlockSpec(memory_space=pltpu.VMEM)
    return pl.pallas_call(
        front_body,
        grid_spec=pltpu.PrefetchScalarGridSpec(
            num_scalar_prefetch=1,
            grid=(samples // block,),
            in_specs=[pl.BlockSpec((block, width_in), lambda i, p: (i, 0)), resident, resident],
            out_specs=[resident, resident, resident],
        ),
        out_shape=[
            pltpu.VMEM((samples, local_hidden), jnp.float32),
            jax.ShapeDtypeStruct((SUBLANES, samples), jnp.float32),
            pltpu.VMEM((replicas, rows, samples), jnp.bfloat16),
        ],
        cost_estimate=pl.CostEstimate(
            flops=2 * samples * width_in * local_hidden,
            bytes_accessed=samples * width_in * 2,
            transcendentals=samples * local_hidden,
        ),
        compiler_params=pltpu.CompilerParams(vmem_limit_bytes=20 * MIB),
        name="front",
    )(place, features, shared_weight, heads)


def errors_body(
    total_samples, one_ref, two_ref, labels_ref, masks_ref, _turned, _slope, errors_ref, losses_ref, *_held
):
    tasks = labels_ref.shape[0]
    logits = (one_ref[...] + two_ref[...])[:tasks]
    targets = labels_ref[...].astype(jnp.float32)
    masks = masks_ref[...].astype(jnp.float32)
    errors_ref[...] = jnp.zeros_like(errors_ref)
    errors_ref[:tasks] = masks * (jax.nn.sigmoid(logits) - targets)
    softplus = jnp.maximum(logits, 0.0) + jnp.log1p(jnp.exp(-jnp.abs(logits)))
    losses = masks * (softplus - targets * logits) / total_samples
    losses_ref[...] = jnp.zeros_like(losses_ref)
    losses_ref[:tasks] = jnp.broadcast_to(
        jnp.sum(losses, axis=1, keepdims=True), (tasks, LANES)
    )


def task_errors(one, two, labels, masks, turned, slope, total_samples):
    resident = pl.BlockSpec(memory_space=pltpu.VMEM)
    return pl.pallas_call(
        functools.partial(errors_body, total_samples),
        in_specs=[resident] * 6,
        out_specs=[resident] * 4,
        out_shape=[
            jax.ShapeDtypeStruct(one.shape, jnp.float32),
            jax.ShapeDtypeStruct((SUBLANES, LANES), jnp.float32),
            pltpu.VMEM(turned.shape, turned.dtype),
            pltpu.VMEM(slope.shape, slope.dtype),
        ],
        input_output_aliases={4: 2, 5: 3},
        compiler_params=pltpu.CompilerParams(vmem_limit_bytes=8 * MIB),
        name="errors",
    )(one, two, labels, masks, turned, slope)


def task_body(
    order, task, wide, turned_ref, slope_ref, errors_ref, heads_ref, send_ref, keep_ref, *rest
):
    terms = rest[-1]
    blocks, rows, depth = turned_ref.shape
    head = heads_ref[task : task + 1].astype(jnp.float32)
    size = min(1024, depth)

    def fill(piece, carry):
        here = pl.ds(pl.multiple_of(piece * size, size), size)
        column = errors_ref[:, here].T[:, task : task + 1]
        terms[here] = ((column * slope_ref[here]) * head).astype(jnp.bfloat16)
        return carry

    lax.fori_loop(0, depth // size, fill, 0)
    ranked = sorted(range(blocks), key=lambda block: [block >> bit & 1 for bit in order])
    half = blocks // 2

    def multiply(tile, carry):
        columns = pl.ds(pl.multiple_of(tile * wide, wide), wide)
        product = jnp.dot(
            turned_ref[...].reshape(blocks * rows, depth),
            terms[:, columns],
            preferred_element_type=jnp.float32,
        )
        for block in range(blocks):
            spot = ranked.index(block)
            out = keep_ref if spot < half else send_ref
            place = pl.ds(spot % half * rows, rows)
            out[place, columns] = product[block * rows : (block + 1) * rows]
        return carry

    lax.fori_loop(0, terms.shape[1] // wide, multiply, 0)


def task_terms(task, order, turned, slope, errors, heads, wide=256):
    blocks, rows, samples = turned.shape
    width = slope.shape[1]
    half = jax.ShapeDtypeStruct((blocks // 2 * rows, width), jnp.float32)
    resident = pl.BlockSpec(memory_space=pltpu.VMEM)
    return pl.pallas_call(
        functools.partial(task_body, order, task, wide),
        in_specs=[resident] * 4,
        out_specs=[resident] * 4,
        out_shape=[
            half,
            half,
            pltpu.VMEM(turned.shape, turned.dtype),
            pltpu.VMEM(slope.shape, slope.dtype),
        ],
        input_output_aliases={0: 2, 1: 3},
        scratch_shapes=[pltpu.VMEM((samples, width), jnp.bfloat16)],
        cost_estimate=pl.CostEstimate(
            flops=2 * samples * blocks * rows * width,
            bytes_accessed=samples * LANES * 4,
            transcendentals=0,
        ),
        compiler_params=pltpu.CompilerParams(vmem_limit_bytes=16 * MIB),
        name="task",
    )(turned, slope, errors, heads)


def gram_body(tasks, *refs):
    keeps, arrived, losses_ref = refs[:tasks], refs[tasks : 2 * tasks], refs[2 * tasks]
    gradients, packed_ref = refs[2 * tasks + 1 : -1], refs[-1]
    rows, width = keeps[0].shape
    pairs = [(one, two) for one in range(tasks) for two in range(one, tasks)]
    zeros = jnp.zeros((SUBLANES, LANES), jnp.float32)

    def strip(index, sums):
        here = pl.ds(pl.multiple_of(index * SUBLANES, SUBLANES), SUBLANES)
        values = []
        for task in range(tasks):
            value = keeps[task][here] + arrived[task][here]
            gradients[task][here] = value
            values.append(value)
        out = []
        for (one, two), total in zip(pairs, sums):
            product = values[one] * values[two]
            for tile in range(width // LANES):
                total = total + product[:, tile * LANES : (tile + 1) * LANES]
            out.append(total)
        return tuple(out)

    sums = lax.fori_loop(0, rows // SUBLANES, strip, (zeros,) * len(pairs))
    row = lax.broadcasted_iota(jnp.int32, (SUBLANES, LANES), 0)
    lane = lax.broadcasted_iota(jnp.int32, (SUBLANES, LANES), 1)
    packed = zeros
    for (one, two), total in zip(pairs, sums):
        value = jnp.sum(total, keepdims=True)
        spots = ((row == one) & (lane == two)) | ((row == two) & (lane == one))
        if one == two:
            spots = spots | ((row == tasks + 1) & (lane == one))
        packed = jnp.where(spots, value, packed)
    for task in range(tasks):
        value = losses_ref[task : task + 1, :1]
        packed = jnp.where((row == tasks) & (lane == task), value, packed)
    packed_ref[...] = jnp.broadcast_to(packed[None], packed_ref.shape)


def gram_terms(keeps, arrived, losses, devices):
    tasks = len(keeps)
    piece = jax.ShapeDtypeStruct(keeps[0].shape, jnp.float32)
    resident = pl.BlockSpec(memory_space=pltpu.VMEM)
    found = pl.pallas_call(
        functools.partial(gram_body, tasks),
        in_specs=[resident] * (2 * tasks + 1),
        out_specs=[resident] * (tasks + 1),
        out_shape=[piece] * tasks
        + [jax.ShapeDtypeStruct((devices, SUBLANES, LANES), jnp.float32)],
        compiler_params=pltpu.CompilerParams(vmem_limit_bytes=16 * MIB),
        name="gram",
    )(*keeps, *arrived, losses)
    return found[:-1], found[-1]


def final_body(tasks, entries, shards, shared_ref, weights_ref, initial_ref, *refs):
    gradients, update_ref, fresh_ref = refs[:tasks], refs[-2], refs[-1]
    total = jnp.sum(shared_ref[...], axis=0)
    lane = lax.broadcasted_iota(jnp.int32, (1, LANES), 1)
    live = lane < tasks
    losses = total[tasks : tasks + 1] / shards
    squares = total[tasks + 1 : tasks + 2]
    weights = weights_ref[...]
    root_mean = jnp.sqrt(squares / entries + epsilon)
    scaled = weights * root_mean
    average = jnp.sum(jnp.where(live, scaled, 0.0), axis=1, keepdims=True) / tasks
    loss_ratio = losses / initial_ref[...]
    relative = loss_ratio / (
        jnp.sum(jnp.where(live, loss_ratio, 0.0), axis=1, keepdims=True) / tasks
    )
    target = average * (relative * jnp.sqrt(relative))
    distance = (scaled - target) / average
    raised = jnp.where(live, weights * jnp.exp(-learn_rate * distance), 0.0)
    fresh = tasks * raised / jnp.sum(raised, axis=1, keepdims=True)
    inner = jnp.sum(total * fresh, axis=1, keepdims=True)
    each = [fresh[:, task : task + 1] for task in range(tasks)]
    mean_square = sum(each[task] * inner[task : task + 1] for task in range(tasks)) / entries
    scale = lax.rsqrt(mean_square + epsilon)
    combined = each[0] * gradients[0][...]
    for task in range(1, tasks):
        combined = combined + each[task] * gradients[task][...]
    update_ref[...] = combined * scale
    fresh_ref[...] = jnp.broadcast_to(fresh, fresh_ref.shape)


def final_terms(shared, weights, initial, gradients, entries, shards):
    tasks = len(gradients)
    resident = pl.BlockSpec(memory_space=pltpu.VMEM)
    spare = ((0, 0), (0, LANES - tasks))
    return pl.pallas_call(
        functools.partial(final_body, tasks, entries, shards),
        in_specs=[resident] * (3 + tasks),
        out_specs=[resident] * 2,
        out_shape=[
            jax.ShapeDtypeStruct(gradients[0].shape, jnp.float32),
            jax.ShapeDtypeStruct((SUBLANES, LANES), jnp.float32),
        ],
        compiler_params=pltpu.CompilerParams(vmem_limit_bytes=16 * MIB),
        name="final",
    )(
        shared,
        jnp.pad(weights[None], spare, constant_values=1.0),
        jnp.pad(initial[None], spare, constant_values=1.0),
        *gradients,
    )


def on_device(
    features, shared_weight, task_heads, labels, task_masks, task_weights, initial_losses
):
    shard_count = lax.axis_size("shard")
    replica_count = lax.axis_size("dp")
    sample_count, width_in = features.shape
    local_hidden = shared_weight.shape[1]
    task_count = task_heads.shape[0]
    entries = width_in * local_hidden * shard_count
    total_samples = sample_count * replica_count
    bits = replica_count.bit_length() - 1
    heads = jnp.pad(task_heads, ((0, LANES - task_count), (0, 0)))
    place = lax.axis_index("dp").astype(jnp.int32).reshape(1)
    slope, logits, turned = front(place, pltpu.with_memory_space_constraint(features, pltpu.HBM), shared_weight, heads, replica_count)
    received = jnp.zeros_like(logits)
    for bit in range(shard_count.bit_length() - 1):
        logits = logits + received if bit else logits
        received = lax.ppermute(logits, "shard", xor_pairs(shard_count, bit))
    errors, losses, turned, slope = task_errors(
        logits, received, labels.T, task_masks.T, turned, slope, total_samples
    )
    keeps, arrived = [], []
    for task, order in enumerate(split_orders(bits, task_count)):
        send, keep, turned, slope = task_terms(task, order, turned, slope, errors, heads)
        for step, bit in enumerate(order):
            received = lax.ppermute(send, "dp", xor_pairs(replica_count, bit))
            if step < bits - 1:
                half = keep.shape[0] // 2
                send = keep[half:] + received[half:]
                keep = keep[:half] + received[:half]
        keeps.append(keep)
        arrived.append(received)
    devices = replica_count * shard_count
    gradients, packed = gram_terms(keeps, arrived, losses, devices)
    shared = lax.all_to_all(packed, ("dp", "shard"), 0, 0)
    update, fresh = final_terms(
        shared, task_weights, initial_losses, gradients, entries, shard_count
    )
    return (update, fresh[0, :task_count])


def solution(mesh):
    return jax.shard_map(
        on_device,
        mesh=mesh,
        in_specs=(
            P("dp", None),
            P(None, "shard"),
            P(None, "shard"),
            P("dp", None),
            P("dp", None),
            P(),
            P(),
        ),
        out_specs=(P("dp", "shard"), P()),
        check_vma=False,
    )
```

time: 676 us -> 299 us (0.44)
  waiting for transfers between devices: 318 us -> 152 us
  matrix products: 102 us -> 0 us
  Pallas kernels: 0 us -> 94.9 us
  other arithmetic: 103 us -> 10.3 us
  blocking collectives: 83.4 us -> 0 us
  local copies, waits for them, and re-layouts: 52.4 us -> 2.87 us
  starting transfers between devices: 0.26 us -> 37.8 us
  between operations: 16.1 us -> 0.93 us
    unnamed x3 -> x0, waiting for transfers between devices: 315 us -> none
    ppermute x0 -> x25, waiting for transfers between devices: none -> 144 us  [the longest x24 143 us: on_device(): received = lax.ppermute(send, 'dp', xor_pairs(replica_count, bit))]
    dot_general x6 -> x0, matrix products: 102 us -> none  [the longest x1 60.6 us: task_term(): lax.dot_general(inputs, terms, (((0,), (0,)), ((), ())), preferred_elemen...]
    pallas_call x0 -> x10, Pallas kernels: none -> 94.9 us  [the longest x6 75.5 us: task_terms(): pl.pallas_call(functools.partial(task_body, order, task, wide), in_specs=...]
    psum x2 -> x0, blocking collectives: 83.4 us -> none  [the longest x1 44.1 us: on_device(): losses = lax.psum(loss_part, 'dp')]
    mul x2 -> x0, other arithmetic: 50.5 us -> none  [the longest x1 49.7 us: on_device(): errors[:, :, None] * silu_slope[:, None, :]]
    convert_element_type x1 -> x0, other arithmetic: 48.2 us -> none  [on_device(): back_terms = (errors[:, :, None] * silu_slope[:, None, :] * task_heads.as...]
    ppermute x0 -> x25, starting transfers between devices: none -> 34.1 us  [the longest x24 33.6 us: on_device(): received = lax.ppermute(send, 'dp', xor_pairs(replica_count, bit))]
  transfers between devices with their start and end apart: 2 -> 26, of which waited for: 2 -> 18; matrix products, arithmetic and copies ran while one was open for 3% -> 3% of each run, Pallas kernels for 0% -> 21%
where the time goes in v1:
time: 299 us
  waiting for transfers between devices  152 us (51%)
  Pallas kernels  94.9 us (32%)
  starting transfers between devices  37.8 us (13%)
  other arithmetic  10.3 us (3%)
    ppermute x24, waiting for transfers between devices, on_device(): received = lax.ppermute(send, 'dp', xor_pairs(replica_count, bit))  143 us
    pallas_call x6, Pallas kernels, task_terms(): pl.pallas_call(functools.partial(task_body, order, task, wide), in_specs=...  75.5 us
    ppermute x24, starting transfers between devices, on_device(): received = lax.ppermute(send, 'dp', xor_pairs(replica_count, bit))  33.6 us
    pallas_call x1, Pallas kernels, front(): pl.pallas_call(front_body, grid_spec=pltpu.PrefetchScalarGridSpec(num_sca...  16.6 us
    add x12, other arithmetic, on_device(): keep = keep[:half] + received[:half]  9.96 us
    all_to_all x1, waiting for transfers between devices, on_device(): shared = lax.all_to_all(packed, ('dp', 'shard'), 0, 0)  8.16 us
  transfers between devices with their start and end apart: 26, of which 18 were waited for; matrix products, arithmetic and copies ran while one was open for 3% of the time, Pallas kernels for 21%

profile of v1, /device:TPU:0, one launch (start us, length us, event | category | flops | bytes accessed | tf_op | source)
XLA Modules:
  0.0 299.0 jit_solution(11894521322936054249)
XLA Ops:
  0.6 0.7 pad.11.heads_ref
  1.4 1.6 copy-done.2
  3.0 16.6 %front.1 = (f32[4096,1024]{1,0:T(8,128)S(1)}, f32[8,4096]{1,0:T(8,128)S(1)}, bf16[16,64,4096]{2,1,0:T(8,128)(2,1)S(1)}) custom-call(s32[1]{0:T(128)} %bitcast.place_ref, bf16[4096,1024]{1,0:T(8,128)(2,1)} %x_ref.1, bf16[1024,1024]{1,0:T(8,128)(2,1)S(1)} %copy-done.2, bf16[128,1024]{1,0:T(8,128)(2,1)S(1)} %pad.11.heads_ref), custom_call_target="tpu_custom_call" | custom-call | flops 8589934592 | bytes 8388608 | tf_op jit(solution)/shard_map/front/pallas_call | solution.py:57
  19.6 0.6 collective-permute-start
  20.1 1.0 collective-permute-done.two_ref
  21.1 0.2 errors.1
  21.3 11.9 %task.6 = (f32[512,1024]{1,0:T(8,128)S(1)}, f32[512,1024]{1,0:T(8,128)S(1)}, bf16[16,64,4096]{2,1,0:T(8,128)(2,1)S(1)}, f32[4096,1024]{1,0:T(8,128)S(1)}) custom-call(bf16[16,64,4096]{2,1,0:T(8,128)(2,1)S(1)} %get-tuple-element.43.turned_ref, f32[4096,1024]{1,0:T(8,128)S(1)} %get-tuple-element.44.slope_ref, ...), custom_call_target="tpu_custom_call", output_to_operand_aliasing={{2}: (0, {}), {3}: (1, {})} | custom-call | flops 8589934592 | bytes 2097152 | tf_op jit(solution)/shard_map/task/pallas_call | solution.py:155
  33.2 2.9 collective-permute-start.1
  36.2 13.2 %task.7 = (f32[512,1024]{1,0:T(8,128)}, f32[512,1024]{1,0:T(8,128)S(1)}, bf16[16,64,4096]{2,1,0:T(8,128)(2,1)S(1)}, f32[4096,1024]{1,0:T(8,128)S(1)}) custom-call(bf16[16,64,4096]{2,1,0:T(8,128)(2,1)S(1)} %get-tuple-element.48.turned_ref, f32[4096,1024]{1,0:T(8,128)S(1)} %get-tuple-element.49.slope_ref, ...), custom_call_target="tpu_custom_call", output_to_operand_aliasing={{2}: (0, {}), {3}: (1, {})} | custom-call | flops 8589934592 | bytes 2097152 | tf_op jit(solution)/shard_map/task/pallas_call | solution.py:155
  49.4 1.5 collective-permute-start.4
  50.9 13.2 %task.8 = (f32[512,1024]{1,0:T(8,128)}, f32[512,1024]{1,0:T(8,128)S(1)}, bf16[16,64,4096]{2,1,0:T(8,128)(2,1)S(1)}, f32[4096,1024]{1,0:T(8,128)S(1)}) custom-call(bf16[16,64,4096]{2,1,0:T(8,128)(2,1)S(1)} %get-tuple-element.52.turned_ref, f32[4096,1024]{1,0:T(8,128)S(1)} %get-tuple-element.53.slope_ref, ...), custom_call_target="tpu_custom_call", output_to_operand_aliasing={{2}: (0, {}), {3}: (1, {})} | custom-call | flops 8589934592 | bytes 2097152 | tf_op jit(solution)/shard_map/task/pallas_call | solution.py:155
  64.1 1.6 collective-permute-start.7
  65.7 13.2 %task.9 = (f32[512,1024]{1,0:T(8,128)}, f32[512,1024]{1,0:T(8,128)S(1)}, bf16[16,64,4096]{2,1,0:T(8,128)(2,1)S(1)}, f32[4096,1024]{1,0:T(8,128)S(1)}) custom-call(bf16[16,64,4096]{2,1,0:T(8,128)(2,1)S(1)} %get-tuple-element.56.turned_ref, f32[4096,1024]{1,0:T(8,128)S(1)} %get-tuple-element.57.slope_ref, ...), custom_call_target="tpu_custom_call", output_to_operand_aliasing={{2}: (0, {}), {3}: (1, {})} | custom-call | flops 8589934592 | bytes 2097152 | tf_op jit(solution)/shard_map/task/pallas_call | solution.py:155
  78.9 0.5 collective-permute-start.10
  79.4 12.1 %task.10 = (f32[512,1024]{1,0:T(8,128)S(1)}, f32[512,1024]{1,0:T(8,128)S(1)}, bf16[16,64,4096]{2,1,0:T(8,128)(2,1)S(1)}, f32[4096,1024]{1,0:T(8,128)S(1)}) custom-call(bf16[16,64,4096]{2,1,0:T(8,128)(2,1)S(1)} %get-tuple-element.60.turned_ref, f32[4096,1024]{1,0:T(8,128)S(1)} %get-tuple-element.61.slope_ref, ...), custom_call_target="tpu_custom_call", output_to_operand_aliasing={{2}: (0, {}), {3}: (1, {})} | custom-call | flops 8589934592 | bytes 2097152 | tf_op jit(solution)/shard_map/task/pallas_call | solution.py:155
  91.4 0.6 collective-permute-start.13
  92.1 11.9 %task.11 = (f32[512,1024]{1,0:T(8,128)S(1)}, f32[512,1024]{1,0:T(8,128)S(1)}, bf16[16,64,4096]{2,1,0:T(8,128)(2,1)S(1)}, f32[4096,1024]{1,0:T(8,128)S(1)}) custom-call(bf16[16,64,4096]{2,1,0:T(8,128)(2,1)S(1)} %get-tuple-element.64.turned_ref, f32[4096,1024]{1,0:T(8,128)S(1)} %get-tuple-element.65.slope_ref, ...), custom_call_target="tpu_custom_call", output_to_operand_aliasing={{2}: (0, {}), {3}: (1, {})} | custom-call | flops 8589934592 | bytes 2097152 | tf_op jit(solution)/shard_map/task/pallas_call | solution.py:155
  104.0 0.4 slice_add_fusion.11
  104.4 2.0 collective-permute-start.2
  106.4 2.0 slice_add_fusion.9
  108.4 4.5 %collective-permute-done.7 = f32[512,1024]{1,0:T(8,128)} collective-permute-done((f32[512,1024]{1,0:T(8,128)}, f32[512,1024]{1,0:T(8,128)}, u32[]{:S(2)}, u32[]{:S(2)}) %collective-permute-start.7) | collective-permute-done | bytes 2097184 | tf_op jit(solution)/shard_map/ppermute | solution.py:308
  112.9 0.5 collective-permute-start.5
  113.4 2.1 slice_add_fusion.7
  115.5 12.2 %collective-permute-done.10 = f32[512,1024]{1,0:T(8,128)} collective-permute-done((f32[512,1024]{1,0:T(8,128)}, f32[512,1024]{1,0:T(8,128)}, u32[]{:S(2)}, u32[]{:S(2)}) %collective-permute-start.10) | collective-permute-done | bytes 2097184 | tf_op jit(solution)/shard_map/ppermute | solution.py:308
  127.7 2.0 collective-permute-start.8
  129.7 2.1 slice_add_fusion.5
  131.8 11.4 %collective-permute-done.13 = f32[512,1024]{1,0:T(8,128)} collective-permute-done((f32[512,1024]{1,0:T(8,128)S(1)}, f32[512,1024]{1,0:T(8,128)}, u32[]{:S(2)}, u32[]{:S(2)}) %collective-permute-start.13) | collective-permute-done | bytes 2097184 | tf_op jit(solution)/shard_map/ppermute | solution.py:308
  143.1 1.5 collective-permute-start.11
  144.6 2.1 slice_add_fusion.3
  146.7 9.6 %collective-permute-done.16 = f32[512,1024]{1,0:T(8,128)S(1)} collective-permute-done((f32[512,1024]{1,0:T(8,128)S(1)}, f32[512,1024]{1,0:T(8,128)S(1)}, u32[]{:S(2)}, u32[]{:S(2)}) %collective-permute-start.16) | collective-permute-done | bytes 2097184 | tf_op jit(solution)/shard_map/ppermute | solution.py:308
  156.4 0.5 collective-permute-start.14
  156.9 0.4 slice_add_fusion.1
  157.3 8.2 %collective-permute-done.2 = f32[256,1024]{1,0:T(8,128)S(1)} collective-permute-done((f32[256,1024]{1,0:T(8,128)S(1)}, f32[256,1024]{1,0:T(8,128)S(1)}, u32[]{:S(2)}, u32[]{:S(2)}) %collective-permute-start.2) | collective-permute-done | bytes 1048608 | tf_op jit(solution)/shard_map/ppermute | solution.py:308
  165.5 1.5 collective-permute-start.17
  167.0 0.2 slice_add_fusion.23
  167.2 1.6 collective-permute-start.3
  168.8 0.2 slice_add_fusion.21
  169.0 3.6 %collective-permute-done.8 = f32[256,1024]{1,0:T(8,128)S(1)} collective-permute-done((f32[256,1024]{1,0:T(8,128)S(1)}, f32[256,1024]{1,0:T(8,128)S(1)}, u32[]{:S(2)}, u32[]{:S(2)}) %collective-permute-start.8) | collective-permute-done | bytes 1048608 | tf_op jit(solution)/shard_map/ppermute | solution.py:308
  172.5 2.0 collective-permute-start.6
  174.8 13.2 %collective-permute-done.11 = f32[256,1024]{1,0:T(8,128)S(1)} collective-permute-done((f32[256,1024]{1,0:T(8,128)S(1)}, f32[256,1024]{1,0:T(8,128)S(1)}, u32[]{:S(2)}, u32[]{:S(2)}) %collective-permute-start.11) | collective-permute-done | bytes 1048608 | tf_op jit(solution)/shard_map/ppermute | solution.py:308
  188.0 1.5 collective-permute-start.9
  189.6 4.8 %collective-permute-done.14 = f32[256,1024]{1,0:T(8,128)S(1)} collective-permute-done((f32[256,1024]{1,0:T(8,128)S(1)}, f32[256,1024]{1,0:T(8,128)S(1)}, u32[]{:S(2)}, u32[]{:S(2)}) %collective-permute-start.14) | collective-permute-done | bytes 1048608 | tf_op jit(solution)/shard_map/ppermute | solution.py:308
  194.4 1.8 collective-permute-start.12
  196.4 14.0 %collective-permute-done.17 = f32[256,1024]{1,0:T(8,128)S(1)} collective-permute-done((f32[256,1024]{1,0:T(8,128)S(1)}, f32[256,1024]{1,0:T(8,128)S(1)}, u32[]{:S(2)}, u32[]{:S(2)}) %collective-permute-start.17) | collective-permute-done | bytes 1048608 | tf_op jit(solution)/shard_map/ppermute | solution.py:308
  210.5 1.6 collective-permute-start.15
  212.2 0.6 collective-permute-start.18
  212.8 2.7 collective-permute-start.19
  215.6 5.0 %collective-permute-done.9 = f32[128,1024]{1,0:T(8,128)S(1)} collective-permute-done((f32[128,1024]{1,0:T(8,128)S(1)}, f32[128,1024]{1,0:T(8,128)S(1)}, u32[]{:S(2)}, u32[]{:S(2)}) %collective-permute-start.9) | collective-permute-done | bytes 524320 | tf_op jit(solution)/shard_map/ppermute | solution.py:308
  220.6 2.6 collective-permute-start.20
  223.3 0.4 collective-permute-start.21
  223.7 6.3 %collective-permute-done.15 = f32[128,1024]{1,0:T(8,128)S(1)} collective-permute-done((f32[128,1024]{1,0:T(8,128)S(1)}, f32[128,1024]{1,0:T(8,128)S(1)}, u32[]{:S(2)}, u32[]{:S(2)}) %collective-permute-start.15) | collective-permute-done | bytes 524320 | tf_op jit(solution)/shard_map/ppermute | solution.py:308
  230.0 0.6 collective-permute-start.22
  230.7 2.4 collective-permute-start.23
  233.2 0.6 collective-permute-start.24
  233.8 28.6 %collective-permute-done.20.refs_7_ = f32[64,1024]{1,0:T(8,128)S(1)} collective-permute-done((f32[64,1024]{1,0:T(8,128)S(1)}, f32[64,1024]{1,0:T(8,128)S(1)}, u32[]{:S(2)}, u32[]{:S(2)}) %collective-permute-start.20) | collective-permute-done | bytes 262176 | tf_op jit(solution)/shard_map/ppermute | solution.py:308
  262.5 5.6 %collective-permute-done.21.refs_8_ = f32[64,1024]{1,0:T(8,128)S(1)} collective-permute-done((f32[64,1024]{1,0:T(8,128)S(1)}, f32[64,1024]{1,0:T(8,128)S(1)}, u32[]{:S(2)}, u32[]{:S(2)}) %collective-permute-start.21) | collective-permute-done | bytes 262176 | tf_op jit(solution)/shard_map/ppermute | solution.py:308
  268.1 5.6 %collective-permute-done.22.refs_9_ = f32[64,1024]{1,0:T(8,128)S(1)} collective-permute-done((f32[64,1024]{1,0:T(8,128)S(1)}, f32[64,1024]{1,0:T(8,128)S(1)}, u32[]{:S(2)}, u32[]{:S(2)}) %collective-permute-start.22) | collective-permute-done | bytes 262176 | tf_op jit(solution)/shard_map/ppermute | solution.py:308
  273.7 5.6 %collective-permute-done.23.refs_10_ = f32[64,1024]{1,0:T(8,128)S(1)} collective-permute-done((f32[64,1024]{1,0:T(8,128)S(1)}, f32[64,1024]{1,0:T(8,128)S(1)}, u32[]{:S(2)}, u32[]{:S(2)}) %collective-permute-start.23) | collective-permute-done | bytes 262176 | tf_op jit(solution)/shard_map/ppermute | solution.py:308
  279.3 4.6 %collective-permute-done.24.refs_11_ = f32[64,1024]{1,0:T(8,128)S(1)} collective-permute-done((f32[64,1024]{1,0:T(8,128)S(1)}, f32[64,1024]{1,0:T(8,128)S(1)}, u32[]{:S(2)}, u32[]{:S(2)}) %collective-permute-start.24) | collective-permute-done | bytes 262176 | tf_op jit(solution)/shard_map/ppermute | solution.py:308
  284.0 1.3 gram.1
  285.3 3.7 %all-to-all-start = ((f32[32,8,128]{2,1,0:T(8,128)}), f32[32,8,128]{2,1,0:T(8,128)S(1)}, u32[]{:S(2)}, u32[]{:S(2)}) async-start(f32[32,8,128]{2,1,0:T(8,128)} %get-tuple-element.69), calls=%async_computation | async-start | bytes 262144 | tf_op jit(solution)/shard_map/all_to_all | solution.py:317
  289.0 8.2 %all-to-all-done.shared_ref = f32[32,8,128]{2,1,0:T(8,128)S(1)} async-done(((f32[32,8,128]{2,1,0:T(8,128)}), f32[32,8,128]{2,1,0:T(8,128)S(1)}, u32[]{:S(2)}, u32[]{:S(2)}) %all-to-all-start) | async-done | bytes 131104 | tf_op jit(solution)/shard_map/all_to_all | solution.py:317
  297.2 1.3 final.1
  298.5 0.5 slice_bitcast_fusion
  (30 shorter events, 1.1 us)
Async XLA Ops:
  1.4 1.6 copy-start.2
  3.0 18.1 %copy-start = (s32[4096,6]{0,1:T(8,128)S(1)}, s32[4096,6]{0,1:T(8,128)}, u32[]{:S(2)}) copy-start(s32[4096,6]{0,1:T(8,128)} %param.10) | copy-start | bytes 294916
  3.0 18.1 %copy-start.1 = (s32[4096,6]{0,1:T(8,128)S(1)}, s32[4096,6]{0,1:T(8,128)}, u32[]{:S(2)}) copy-start(s32[4096,6]{0,1:T(8,128)} %param.11) | copy-start | bytes 294916
  19.6 1.5 collective-permute-start
  33.2 70.7 %collective-permute-start.1 = (f32[512,1024]{1,0:T(8,128)S(1)}, f32[512,1024]{1,0:T(8,128)S(1)}, u32[]{:S(2)}, u32[]{:S(2)}) collective-permute-start(f32[512,1024]{1,0:T(8,128)S(1)} %get-tuple-element.47), channel_id=1, source_target_pairs={{0,4},{2,6},{4,0},{6,2},{8,12},{10,14},{12,8},{14,10},{16,20},{18,... | collective-permute-start | bytes 6291464 | tf_op jit(solution)/shard_map/ppermute | solution.py:308
  49.4 55.0 %collective-permute-start.4 = (f32[512,1024]{1,0:T(8,128)}, f32[512,1024]{1,0:T(8,128)}, u32[]{:S(2)}, u32[]{:S(2)}) collective-permute-start(f32[512,1024]{1,0:T(8,128)} %get-tuple-element.51), channel_id=1, source_target_pairs={{0,2},{2,0},{4,6},{6,4},{8,10},{10,8},{12,14},{14,12},{16,18},{18,... | collective-permute-start | bytes 6291464 | tf_op jit(solution)/shard_map/ppermute | solution.py:308
  64.1 48.8 %collective-permute-start.7 = (f32[512,1024]{1,0:T(8,128)}, f32[512,1024]{1,0:T(8,128)}, u32[]{:S(2)}, u32[]{:S(2)}) collective-permute-start(f32[512,1024]{1,0:T(8,128)} %get-tuple-element.55), channel_id=1, source_target_pairs={{0,8},{2,10},{4,12},{6,14},{8,0},{10,2},{12,4},{14,6},{16,24},{18,... | collective-permute-start | bytes 6291464 | tf_op jit(solution)/shard_map/ppermute | solution.py:308
  78.9 48.8 %collective-permute-start.10 = (f32[512,1024]{1,0:T(8,128)}, f32[512,1024]{1,0:T(8,128)}, u32[]{:S(2)}, u32[]{:S(2)}) collective-permute-start(f32[512,1024]{1,0:T(8,128)} %get-tuple-element.59), channel_id=1, source_target_pairs={{0,4},{2,6},{4,0},{6,2},{8,12},{10,14},{12,8},{14,10},{16,20},{18,... | collective-permute-start | bytes 6291464 | tf_op jit(solution)/shard_map/ppermute | solution.py:308
  91.4 51.7 %collective-permute-start.13 = (f32[512,1024]{1,0:T(8,128)S(1)}, f32[512,1024]{1,0:T(8,128)}, u32[]{:S(2)}, u32[]{:S(2)}) collective-permute-start(f32[512,1024]{1,0:T(8,128)S(1)} %get-tuple-element.63), channel_id=1, source_target_pairs={{0,2},{2,0},{4,6},{6,4},{8,10},{10,8},{12,14},{14,12},{16,18},{18,... | collective-permute-start | bytes 6291464 | tf_op jit(solution)/shard_map/ppermute | solution.py:308
  103.9 52.4 %collective-permute-start.16 = (f32[512,1024]{1,0:T(8,128)S(1)}, f32[512,1024]{1,0:T(8,128)S(1)}, u32[]{:S(2)}, u32[]{:S(2)}) collective-permute-start(f32[512,1024]{1,0:T(8,128)S(1)} %get-tuple-element.67), channel_id=1, source_target_pairs={{0,8},{2,10},{4,12},{6,14},{8,0},{10,2},{12,4},{14,6},{16,24},{18,... | collective-permute-start | bytes 6291464 | tf_op jit(solution)/shard_map/ppermute | solution.py:308
  104.4 61.1 %collective-permute-start.2 = (f32[256,1024]{1,0:T(8,128)S(1)}, f32[256,1024]{1,0:T(8,128)S(1)}, u32[]{:S(2)}, u32[]{:S(2)}) collective-permute-start(f32[256,1024]{1,0:T(8,128)S(1)} %get-tuple-element.89), channel_id=1, source_target_pairs={{0,2},{2,0},{4,6},{6,4},{8,10},{10,8},{12,14},{14,12},{16,18},{18,... | collective-permute-start | bytes 3145736 | tf_op jit(solution)/shard_map/ppermute | solution.py:308
  112.9 54.2 %collective-permute-start.5 = (f32[256,1024]{1,0:T(8,128)S(1)}, f32[256,1024]{1,0:T(8,128)S(1)}, u32[]{:S(2)}, u32[]{:S(2)}) collective-permute-start(f32[256,1024]{1,0:T(8,128)S(1)} %get-tuple-element.87), channel_id=1, source_target_pairs={{0,4},{2,6},{4,0},{6,2},{8,12},{10,14},{12,8},{14,10},{16,20},{18,... | collective-permute-start | bytes 3145736 | tf_op jit(solution)/shard_map/ppermute | solution.py:308
  127.7 44.8 %collective-permute-start.8 = (f32[256,1024]{1,0:T(8,128)S(1)}, f32[256,1024]{1,0:T(8,128)S(1)}, u32[]{:S(2)}, u32[]{:S(2)}) collective-permute-start(f32[256,1024]{1,0:T(8,128)S(1)} %get-tuple-element.85), channel_id=1, source_target_pairs={{0,4},{2,6},{4,0},{6,2},{8,12},{10,14},{12,8},{14,10},{16,20},{18,... | collective-permute-start | bytes 3145736 | tf_op jit(solution)/shard_map/ppermute | solution.py:308
  143.1 44.8 %collective-permute-start.11 = (f32[256,1024]{1,0:T(8,128)S(1)}, f32[256,1024]{1,0:T(8,128)S(1)}, u32[]{:S(2)}, u32[]{:S(2)}) collective-permute-start(f32[256,1024]{1,0:T(8,128)S(1)} %get-tuple-element.83), channel_id=1, source_target_pairs={{0,2},{2,0},{4,6},{6,4},{8,10},{10,8},{12,14},{14,12},{16,18},{18,... | collective-permute-start | bytes 3145736 | tf_op jit(solution)/shard_map/ppermute | solution.py:308
  156.4 38.1 %collective-permute-start.14 = (f32[256,1024]{1,0:T(8,128)S(1)}, f32[256,1024]{1,0:T(8,128)S(1)}, u32[]{:S(2)}, u32[]{:S(2)}) collective-permute-start(f32[256,1024]{1,0:T(8,128)S(1)} %get-tuple-element.81), channel_id=1, source_target_pairs={{0,4},{2,6},{4,0},{6,2},{8,12},{10,14},{12,8},{14,10},{16,20},{18,... | collective-permute-start | bytes 3145736 | tf_op jit(solution)/shard_map/ppermute | solution.py:308
  165.5 44.9 %collective-permute-start.17 = (f32[256,1024]{1,0:T(8,128)S(1)}, f32[256,1024]{1,0:T(8,128)S(1)}, u32[]{:S(2)}, u32[]{:S(2)}) collective-permute-start(f32[256,1024]{1,0:T(8,128)S(1)} %get-tuple-element.79), channel_id=1, source_target_pairs={{0,2},{2,0},{4,6},{6,4},{8,10},{10,8},{12,14},{14,12},{16,18},{18,... | collective-permute-start | bytes 3145736 | tf_op jit(solution)/shard_map/ppermute | solution.py:308
  167.2 45.0 %collective-permute-start.3 = (f32[128,1024]{1,0:T(8,128)S(1)}, f32[128,1024]{1,0:T(8,128)S(1)}, u32[]{:S(2)}, u32[]{:S(2)}) collective-permute-start(f32[128,1024]{1,0:T(8,128)S(1)} %get-tuple-element.101), channel_id=1, source_target_pairs={{0,8},{2,10},{4,12},{6,14},{8,0},{10,2},{12,4},{14,6},{16,24},{18,... | collective-permute-start | bytes 1572872 | tf_op jit(solution)/shard_map/ppermute | solution.py:308
  172.5 40.3 %collective-permute-start.6 = (f32[128,1024]{1,0:T(8,128)S(1)}, f32[128,1024]{1,0:T(8,128)S(1)}, u32[]{:S(2)}, u32[]{:S(2)}) collective-permute-start(f32[128,1024]{1,0:T(8,128)S(1)} %get-tuple-element.99), channel_id=1, source_target_pairs={{0,8},{2,10},{4,12},{6,14},{8,0},{10,2},{12,4},{14,6},{16,24},{18,... | collective-permute-start | bytes 1572872 | tf_op jit(solution)/shard_map/ppermute | solution.py:308
  188.0 32.6 %collective-permute-start.9 = (f32[128,1024]{1,0:T(8,128)S(1)}, f32[128,1024]{1,0:T(8,128)S(1)}, u32[]{:S(2)}, u32[]{:S(2)}) collective-permute-start(f32[128,1024]{1,0:T(8,128)S(1)} %get-tuple-element.97), channel_id=1, source_target_pairs={{0,2},{2,0},{4,6},{6,4},{8,10},{10,8},{12,14},{14,12},{16,18},{18,... | collective-permute-start | bytes 1572872 | tf_op jit(solution)/shard_map/ppermute | solution.py:308
  194.4 28.8 %collective-permute-start.12 = (f32[128,1024]{1,0:T(8,128)S(1)}, f32[128,1024]{1,0:T(8,128)S(1)}, u32[]{:S(2)}, u32[]{:S(2)}) collective-permute-start(f32[128,1024]{1,0:T(8,128)S(1)} %get-tuple-element.95), channel_id=1, source_target_pairs={{0,8},{2,10},{4,12},{6,14},{8,0},{10,2},{12,4},{14,6},{16,24},{18,... | collective-permute-start | bytes 1572872 | tf_op jit(solution)/shard_map/ppermute | solution.py:308
  210.5 19.6 %collective-permute-start.15 = (f32[128,1024]{1,0:T(8,128)S(1)}, f32[128,1024]{1,0:T(8,128)S(1)}, u32[]{:S(2)}, u32[]{:S(2)}) collective-permute-start(f32[128,1024]{1,0:T(8,128)S(1)} %get-tuple-element.93), channel_id=1, source_target_pairs={{0,8},{2,10},{4,12},{6,14},{8,0},{10,2},{12,4},{14,6},{16,24},{18,... | collective-permute-start | bytes 1572872 | tf_op jit(solution)/shard_map/ppermute | solution.py:308
  212.2 18.5 %collective-permute-start.18 = (f32[128,1024]{1,0:T(8,128)S(1)}, f32[128,1024]{1,0:T(8,128)S(1)}, u32[]{:S(2)}, u32[]{:S(2)}) collective-permute-start(f32[128,1024]{1,0:T(8,128)S(1)} %get-tuple-element.91), channel_id=1, source_target_pairs={{0,4},{2,6},{4,0},{6,2},{8,12},{10,14},{12,8},{14,10},{16,20},{18,... | collective-permute-start | bytes 1572872 | tf_op jit(solution)/shard_map/ppermute | solution.py:308
  212.8 20.3 %collective-permute-start.19 = (f32[64,1024]{1,0:T(8,128)S(1)}, f32[64,1024]{1,0:T(8,128)S(1)}, u32[]{:S(2)}, u32[]{:S(2)}) collective-permute-start(f32[64,1024]{1,0:T(8,128)S(1)} %get-tuple-element.112), channel_id=1, source_target_pairs={{0,16},{2,18},{4,20},{6,22},{8,24},{10,26},{12,28},{14,30},{16,0},... | collective-permute-start | bytes 786440 | tf_op jit(solution)/shard_map/ppermute | solution.py:308
  220.6 41.9 %collective-permute-start.20 = (f32[64,1024]{1,0:T(8,128)S(1)}, f32[64,1024]{1,0:T(8,128)S(1)}, u32[]{:S(2)}, u32[]{:S(2)}) collective-permute-start(f32[64,1024]{1,0:T(8,128)S(1)} %get-tuple-element.110), channel_id=1, source_target_pairs={{0,16},{2,18},{4,20},{6,22},{8,24},{10,26},{12,28},{14,30},{16,0},... | collective-permute-start | bytes 786440 | tf_op jit(solution)/shard_map/ppermute | solution.py:308
  223.3 44.8 %collective-permute-start.21 = (f32[64,1024]{1,0:T(8,128)S(1)}, f32[64,1024]{1,0:T(8,128)S(1)}, u32[]{:S(2)}, u32[]{:S(2)}) collective-permute-start(f32[64,1024]{1,0:T(8,128)S(1)} %get-tuple-element.108), channel_id=1, source_target_pairs={{0,16},{2,18},{4,20},{6,22},{8,24},{10,26},{12,28},{14,30},{16,0},... | collective-permute-start | bytes 786440 | tf_op jit(solution)/shard_map/ppermute | solution.py:308
  230.0 43.7 %collective-permute-start.22 = (f32[64,1024]{1,0:T(8,128)S(1)}, f32[64,1024]{1,0:T(8,128)S(1)}, u32[]{:S(2)}, u32[]{:S(2)}) collective-permute-start(f32[64,1024]{1,0:T(8,128)S(1)} %get-tuple-element.106), channel_id=1, source_target_pairs={{0,16},{2,18},{4,20},{6,22},{8,24},{10,26},{12,28},{14,30},{16,0},... | collective-permute-start | bytes 786440 | tf_op jit(solution)/shard_map/ppermute | solution.py:308
  230.7 48.7 %collective-permute-start.23 = (f32[64,1024]{1,0:T(8,128)S(1)}, f32[64,1024]{1,0:T(8,128)S(1)}, u32[]{:S(2)}, u32[]{:S(2)}) collective-permute-start(f32[64,1024]{1,0:T(8,128)S(1)} %get-tuple-element.104), channel_id=1, source_target_pairs={{0,16},{2,18},{4,20},{6,22},{8,24},{10,26},{12,28},{14,30},{16,0},... | collective-permute-start | bytes 786440 | tf_op jit(solution)/shard_map/ppermute | solution.py:308
  233.2 55.8 %copy-start.3 = (f32[6]{0:T(128)S(1)}, f32[6]{0:T(128)}, u32[]{:S(2)}) copy-start(f32[6]{0:T(128)} %param.12) | copy-start | bytes 76
  233.2 55.9 %copy-start.4 = (f32[6]{0:T(128)S(1)}, f32[6]{0:T(128)}, u32[]{:S(2)}) copy-start(f32[6]{0:T(128)} %param.13) | copy-start | bytes 76
  233.2 50.8 %collective-permute-start.24 = (f32[64,1024]{1,0:T(8,128)S(1)}, f32[64,1024]{1,0:T(8,128)S(1)}, u32[]{:S(2)}, u32[]{:S(2)}) collective-permute-start(f32[64,1024]{1,0:T(8,128)S(1)} %get-tuple-element.102), channel_id=1, source_target_pairs={{0,16},{2,18},{4,20},{6,22},{8,24},{10,26},{12,28},{14,30},{16,0},... | collective-permute-start | bytes 786440 | tf_op jit(solution)/shard_map/ppermute | solution.py:308
  285.3 11.9 %all-to-all-start = ((f32[32,8,128]{2,1,0:T(8,128)}), f32[32,8,128]{2,1,0:T(8,128)S(1)}, u32[]{:S(2)}, u32[]{:S(2)}) async-start(f32[32,8,128]{2,1,0:T(8,128)} %get-tuple-element.69), calls=%async_computation | async-start | bytes 262144 | tf_op jit(solution)/shard_map/all_to_all | solution.py:317
